TPU v7x, 32 devices: a whole 2x2x4 slice. The times are simulated.
32 devices in a mesh: dp: 8 (over z, y), tensor: 4 (over x, core).
Axes of the slice: x: 2, y: 2, z: 4, core: 2. Of those that a mesh axis runs over, the one named last changes fastest.
Arguments:
- hidden_in: bfloat16 [16384, 1024], P(('dp', 'tensor')), may hold values from -6 to 6
- doc_ids: int32 [32, 512], P('dp'), may hold values from 0 to 5, never falling along the last dimension, each value on 1 to 256 neighbouring positions
- unit_slot: int32 [24], replicated, may hold values from 0 to 31, as said below
- masters: float32 [32, 1024, 1024], P('dp', None, 'tensor')
- first_moment: float32 [32, 1024, 1024], P('dp', None, 'tensor')
- second_moment: float32 [32, 1024, 1024], P('dp', None, 'tensor')
- column_state: float32 [3, 2, 6, 1024], P(None, None, None, 'tensor')
- row_state: float32 [3, 2, 6, 1024], replicated
- out_grad: bfloat16 [16384, 1024], P(('dp', 'tensor')), may hold values from -0.046875 to 0.046875
Outputs:
- block_out: float32 [16384, 1024], P(('dp', 'tensor'))
- input_grad: float32 [16384, 1024], P(('dp', 'tensor'))
- unit_master: float32 [32, 1024, 1024], P('dp', None, 'tensor')
- unit_state: float32 [2, 32, 1024, 1024], P(None, 'dp', None, 'tensor')
- column_out: float32 [4, 2, 6, 1024], P(None, None, None, 'tensor')
- row_out: float32 [4, 2, 6, 1024], replicated
Inputs may be any that keep to these rules, and one draw needn't show every extreme that they name: `doc_ids`: within a row the ids never fall; each of the 6 documents covers 1 to 256 tokens, one exactly that many. `unit_slot`: all 24 entries differ; slot s belongs to index s // 4 of dp; some index of dp holds exactly 4 matrices.
All inputs are finite; a program needn't handle non-finite values.
Results may differ from a plain program's by a relative error of at most 0.028.
Values may be sent and summed in bfloat16 or wider, within the bound.
A program may use at most 256 MiB of HBM per device.

v0:
```python
import math
import jax
import jax.numpy as jnp
from jax import lax
from jax.sharding import PartitionSpec as P

HEAD_DIM = 64
LAYERS = 2
STEP = 3
EPS_NORM = 1e-06
RATE_UNITS = 0.05
RATE_SMALL = 0.2
WEIGHT_DECAY = 0.01
ADAM_EPS = 1e-08
BETA_MOMENT = 0.5
BOTH = ("dp", "tensor")


def norm_forward(summed, gain, shift):
    row_mean = jnp.mean(summed, axis=1, keepdims=True)
    centred = summed - row_mean
    inverse = lax.rsqrt(jnp.mean(centred * centred, axis=1, keepdims=True) + EPS_NORM)
    scaled = centred * inverse
    return (scaled * gain + shift, scaled, inverse)


def norm_backward(upstream, scaled, inverse, gain):
    d_scaled = upstream * gain
    mean_one = jnp.mean(d_scaled, axis=1, keepdims=True)
    mean_two = jnp.mean(d_scaled * scaled, axis=1, keepdims=True)
    grad_input = inverse * (d_scaled - mean_one - scaled * mean_two)
    return (grad_input, jnp.sum(upstream * scaled, axis=0), jnp.sum(upstream, axis=0))


def gelu_pair(v):
    z = jnp.abs(v) * 2.0 ** (-0.5)
    t = 1.0 / (1.0 + 0.5 * z)
    poly = 0.17087277
    for coefficient in (
        -0.82215223,
        1.48851587,
        -1.13520398,
        0.27886807,
        -0.18628806,
        0.09678418,
        0.37409196,
        1.00002368,
        -1.26551223,
    ):
        poly = poly * t + coefficient
    bell = jnp.exp(-0.5 * v * v)
    tail = 0.5 * t * jnp.exp(poly) * bell
    cdf = jnp.where(v >= 0.0, 1.0 - tail, tail)
    return (v * cdf, cdf + v * bell * (2.0 * math.pi) ** (-0.5))


def adamw_update(old_value, gradient, first_old, second_old, learn_rate):
    first_new = BETA_MOMENT * first_old + (1.0 - BETA_MOMENT) * gradient
    second_new = BETA_MOMENT * second_old + (1.0 - BETA_MOMENT) * gradient * gradient
    correct = 1.0 - BETA_MOMENT**STEP
    step_size = first_new / correct / (jnp.sqrt(second_new / correct) + ADAM_EPS)
    return (old_value - learn_rate * (step_size + WEIGHT_DECAY * old_value), first_new, second_new)


def dot(left, right, dims):
    return lax.dot_general(left, right, (dims, ((), ())), preferred_element_type=jnp.float32)


def local(
    hidden_in,
    doc_ids,
    unit_slot,
    masters,
    first_moment,
    second_moment,
    column_state,
    row_state,
    out_grad,
):
    slot_count, width, col_width = masters.shape
    units = unit_slot.shape[0]
    per_layer = units // LAYERS
    blocks = (per_layer - 4) // 2
    dp_size = lax.axis_size("dp")
    tensor_size = lax.axis_size("tensor")
    devices = dp_size * tensor_size
    slots = slot_count * dp_size
    rows = hidden_in.shape[0]
    seq_len = doc_ids.shape[1]
    heads = width // HEAD_DIM
    piece = width // devices
    share = seq_len // rows
    tensor_index = lax.axis_index("tensor")
    groups = [list(range(i, i + share)) for i in range(0, tensor_size, share)]
    score_scale = HEAD_DIM ** (-0.5)
    sent = masters.astype(jnp.bfloat16).reshape(slot_count, devices, piece, col_width)
    spread = lax.all_to_all(sent.transpose(1, 0, 2, 3), BOTH, 0, 0)
    spread = spread.reshape(dp_size, tensor_size, slot_count, piece, col_width)
    spread = spread.transpose(0, 2, 3, 1, 4).reshape(slots, piece, width)
    mine = spread[unit_slot]
    layer_mats = []
    for layer in range(LAYERS):
        own = mine[layer * per_layer : (layer + 1) * per_layer].transpose(1, 0, 2)
        full = lax.all_gather(own.reshape(piece, per_layer * width), BOTH, axis=0, tiled=True)
        layer_mats.append(
            (
                full[:, : 3 * width],
                full[:, 3 * width : 4 * width],
                full[:, 4 * width : (4 + blocks) * width],
                full[:, (4 + blocks) * width :],
            )
        )
    row_docs = lax.dynamic_slice_in_dim(doc_ids, tensor_index // share, 1, axis=0)[0]
    my_docs = lax.dynamic_slice_in_dim(row_docs, tensor_index % share * rows, rows)
    same_doc = (my_docs[:, None] == row_docs[None, :])[None]

    def whole_row(value):
        if share == 1:
            return value
        return lax.all_gather(value, "tensor", axis=0, tiled=True, axis_index_groups=groups)

    def own_rows(value):
        if share == 1:
            return value
        return lax.psum_scatter(
            value, "tensor", scatter_dimension=0, tiled=True, axis_index_groups=groups
        )

    col_full = lax.all_gather(column_state[0], "tensor", axis=2, tiled=True)
    hidden = hidden_in.astype(jnp.float32)
    saved_layers = []
    for layer in range(LAYERS):
        w_qkv, w_proj, w_in, w_out = layer_mats[layer]
        row_now = row_state[0, layer]
        col_now = col_full[layer]
        hidden_bf = hidden.astype(jnp.bfloat16)
        mixed = dot(hidden_bf, w_qkv, ((1,), (0,)))
        query = (mixed[:, :width] + col_now[0]).astype(jnp.bfloat16)
        key = whole_row(mixed[:, width : 2 * width].astype(jnp.bfloat16))
        value = whole_row((mixed[:, 2 * width :] + col_now[1]).astype(jnp.bfloat16))
        query = query.reshape(rows, heads, HEAD_DIM)
        key = key.reshape(seq_len, heads, HEAD_DIM)
        value = value.reshape(seq_len, heads, HEAD_DIM)
        scores = (
            jnp.einsum("qhd,khd->hqk", query, key, preferred_element_type=jnp.float32) * score_scale
        )
        scores = jnp.where(same_doc, scores, -1e30)
        row_top = jnp.max(scores, axis=-1, keepdims=True)
        log_total = row_top + jnp.log(jnp.sum(jnp.exp(scores - row_top), axis=-1, keepdims=True))
        soft_bf = jnp.exp(scores - log_total).astype(jnp.bfloat16)
        context = jnp.einsum("hqk,khd->qhd", soft_bf, value, preferred_element_type=jnp.float32)
        context = context.reshape(rows, width).astype(jnp.bfloat16)
        attended = dot(context, w_proj, ((1,), (1,)))
        normed, scaled_one, inverse_one = norm_forward(
            hidden + attended + row_now[0], row_now[2], row_now[3]
        )
        normed_bf = normed.astype(jnp.bfloat16)
        pre_act = dot(normed_bf, w_in, ((1,), (0,))) + col_now[2:].reshape(-1)
        activated, slope = gelu_pair(pre_act)
        activated = activated.astype(jnp.bfloat16)
        slope = slope.astype(jnp.bfloat16)
        mlp_out = dot(activated, w_out, ((1,), (1,)))
        output, scaled_two, inverse_two = norm_forward(
            normed + mlp_out + row_now[1], row_now[4], row_now[5]
        )
        saved_layers.append(
            (hidden_bf, query, key, value, log_total, context, scaled_one, inverse_one, normed_bf)
            + (slope, activated, scaled_two, inverse_two)
        )
        hidden = output
    upstream = out_grad.astype(jnp.float32)
    pieces = [None] * LAYERS
    col_parts = [None] * LAYERS
    row_parts = [None] * LAYERS
    for layer in reversed(range(LAYERS)):
        w_qkv, w_proj, w_in, w_out = layer_mats[layer]
        row_now = row_state[0, layer]
        (
            hidden_bf,
            query,
            key,
            value,
            log_total,
            context,
            scaled_one,
            inverse_one,
            normed_bf,
            slope,
            activated,
            scaled_two,
            inverse_two,
        ) = saved_layers[layer]
        d_two, gain_two, shift_two = norm_backward(upstream, scaled_two, inverse_two, row_now[4])
        grad_bias_two = jnp.sum(d_two, axis=0)
        d_two_bf = d_two.astype(jnp.bfloat16)
        grad_w_out = dot(d_two_bf, activated, ((0,), (0,)))
        d_pre = (dot(d_two_bf, w_out, ((1,), (0,))) * slope).astype(jnp.bfloat16)
        grad_bias_in = jnp.sum(d_pre, axis=0, dtype=jnp.float32)
        grad_w_in = dot(normed_bf, d_pre, ((0,), (0,)))
        d_normed = d_two + dot(d_pre, w_in, ((1,), (1,)))
        d_one, gain_one, shift_one = norm_backward(d_normed, scaled_one, inverse_one, row_now[2])
        grad_bias_proj = jnp.sum(d_one, axis=0)
        d_one_bf = d_one.astype(jnp.bfloat16)
        grad_w_proj = dot(d_one_bf, context, ((0,), (0,)))
        d_context = (
            dot(d_one_bf, w_proj, ((1,), (0,))).astype(jnp.bfloat16).reshape(rows, heads, HEAD_DIM)
        )
        scores = (
            jnp.einsum("qhd,khd->hqk", query, key, preferred_element_type=jnp.float32) * score_scale
        )
        scores = jnp.where(same_doc, scores, -1e30)
        soft = jnp.exp(scores - log_total)
        d_values = jnp.einsum(
            "hqk,qhd->khd", soft.astype(jnp.bfloat16), d_context, preferred_element_type=jnp.float32
        )
        d_probs = jnp.einsum("qhd,khd->hqk", d_context, value, preferred_element_type=jnp.float32)
        d_scores = (soft * (d_probs - jnp.sum(soft * d_probs, axis=-1, keepdims=True))).astype(
            jnp.bfloat16
        )
        d_queries = (
            jnp.einsum("hqk,khd->qhd", d_scores, key, preferred_element_type=jnp.float32)
            * score_scale
        )
        d_keys = (
            jnp.einsum("hqk,qhd->khd", d_scores, query, preferred_element_type=jnp.float32)
            * score_scale
        )
        d_qkv = jnp.concatenate(
            [
                d_queries.reshape(rows, width),
                own_rows(d_keys.reshape(seq_len, width)),
                own_rows(d_values.reshape(seq_len, width)),
            ],
            axis=1,
        ).astype(jnp.bfloat16)
        grad_bias_qkv = jnp.sum(d_qkv, axis=0, dtype=jnp.float32)
        grad_w_qkv = dot(hidden_bf, d_qkv, ((0,), (0,)))
        upstream = d_one + dot(d_qkv, w_qkv, ((1,), (1,)))
        whole = jnp.concatenate([grad_w_qkv, grad_w_proj, grad_w_in, grad_w_out], axis=1)
        pieces[layer] = lax.psum_scatter(
            whole.astype(jnp.bfloat16), BOTH, scatter_dimension=0, tiled=True
        )
        col_parts[layer] = jnp.concatenate(
            [
                grad_bias_qkv[:width][None],
                grad_bias_qkv[2 * width :][None],
                grad_bias_in.reshape(blocks, width),
            ],
            axis=0,
        )
        row_parts[layer] = jnp.stack(
            [grad_bias_proj, grad_bias_two, gain_one, shift_one, gain_two, shift_two]
        )
    small = lax.psum(jnp.stack([jnp.stack(col_parts), jnp.stack(row_parts)]), BOTH)
    row_total = small[1]
    col_total = lax.dynamic_slice_in_dim(small[0], tensor_index * col_width, col_width, axis=2)
    summed = jnp.concatenate(
        [part.reshape(piece, per_layer, width).transpose(1, 0, 2) for part in pieces], axis=0
    )
    slot_ids = jnp.arange(slots, dtype=jnp.int32)
    named = unit_slot[None, :] == slot_ids[:, None]
    holds = jnp.any(named, axis=1)
    unit_of = jnp.argmax(named, axis=1)
    back = jnp.where(holds[:, None, None], summed[unit_of], jnp.zeros((), jnp.bfloat16))
    back = back.reshape(dp_size, slot_count, piece, tensor_size, col_width)
    back = back.transpose(0, 3, 1, 2, 4).reshape(devices, slot_count, piece, col_width)
    owned = lax.all_to_all(back, BOTH, 0, 0)
    owned = owned.transpose(1, 0, 2, 3).reshape(slot_count, width, col_width).astype(jnp.float32)
    occupied = lax.dynamic_slice_in_dim(holds, lax.axis_index("dp") * slot_count, slot_count)
    occupied = occupied.astype(jnp.float32)[:, None, None]
    new_master, new_first, new_second = adamw_update(
        masters, owned, first_moment, second_moment, RATE_UNITS
    )
    unit_master = new_master * occupied
    unit_state = jnp.stack([new_first * occupied, new_second * occupied])
    new_col, col_first, col_second = adamw_update(
        column_state[0], col_total, column_state[1], column_state[2], RATE_SMALL
    )
    column_out = jnp.stack([col_total, new_col, col_first, col_second])
    new_row, row_first, row_second = adamw_update(
        row_state[0], row_total, row_state[1], row_state[2], RATE_SMALL
    )
    row_out = jnp.stack([row_total, new_row, row_first, row_second])
    return (hidden, upstream, unit_master, unit_state, column_out, row_out)


def solution(mesh):
    return jax.shard_map(
        local,
        mesh=mesh,
        in_specs=(
            P(("dp", "tensor"), None),
            P("dp", None),
            P(),
            P("dp", None, "tensor"),
            P("dp", None, "tensor"),
            P("dp", None, "tensor"),
            P(None, None, None, "tensor"),
            P(),
            P(("dp", "tensor"), None),
        ),
        out_specs=(
            P(("dp", "tensor"), None),
            P(("dp", "tensor"), None),
            P("dp", None, "tensor"),
            P(None, "dp", None, "tensor"),
            P(None, None, None, "tensor"),
            P(),
        ),
        check_vma=False,
    )
```

profile of v0, /device:TPU:8, one launch (start us, length us, event | category | flops | bytes accessed | tf_op | source)
XLA Modules:
  0.0 1338.4 jit_solution(5560922566335390330)
XLA Ops:
  17.3 46.5 %all-to-all-done = bf16[32,4,32,256]{3,2,1,0:T(8,128)(2,1)S(1)} async-done(((bf16[32,4,32,256]{3,2,1,0:T(8,128)(2,1)}), bf16[32,4,32,256]{3,2,1,0:T(8,128)(2,1)S(1)}, u32[]{:S(2)}, u32[]{:S(2)}) %all-to-all-start) | async-done | bytes 2097184 | tf_op jit(solution)/shard_map/all_to_all | solution.py:97
  83.2 145.9 %all-gather.4.cloned.1.call-done = bf16[1024,12288]{1,0:T(8,128)(2,1)} async-done(((bf16[32,12288]{1,0:T(8,128)(2,1)}), bf16[1024,12288]{1,0:T(8,128)(2,1)}) %all-gather.4.cloned.1.call-update) | async-done | bytes 25165840 | tf_op jit(solution)/shard_map/all_gather | solution.py:104
  242.9 9.4 exponential_reduce_fusion.1
  264.6 18.3 %multiply_convert_fusion.5 = (bf16[512,4096]{1,0:T(8,128)(2,1)S(1)}, f32[512,4096]{1,0:T(8,128)}) fusion(f32[4096]{0:T(1024)S(1)} %bitcast.236, bf16[1024,12288]{1,0:T(8,128)(2,1)} %all-gather.4.cloned.1.call-done, f32[512,1024]{1,0:T(8,128)S(1)} %get-tuple-element.76, f32[1024]{0:T(1024)S(1)} %bitcast.252, f32[1024]{0:T(1024)S(1)} %bitcast.222, ...), kind=kOutput, calls=%fused_computation.40 | convolution fusion | flops 4366794752 | bytes 23097344 | tf_op jit(solution)/shard_map/dot_general | solution.py:66
  283.0 8.7 fusion.138
  292.1 93.3 %all-gather.6.cloned.1.call-done = bf16[1024,12288]{1,0:T(8,128)(2,1)} async-done(((bf16[32,12288]{1,0:T(8,128)(2,1)}), bf16[1024,12288]{1,0:T(8,128)(2,1)}) %all-gather.6.cloned.1.call-update) | async-done | bytes 25165840 | tf_op jit(solution)/shard_map/all_gather | solution.py:104
  401.8 9.5 exponential_reduce_fusion
  424.4 18.3 %multiply_convert_fusion.4 = (bf16[512,4096]{1,0:T(8,128)(2,1)S(1)}, f32[512,4096]{1,0:T(8,128)}) fusion(f32[4096]{0:T(1024)S(1)} %bitcast.238, bf16[1024,12288]{1,0:T(8,128)(2,1)} %all-gather.6.cloned.1.call-done, f32[512,1024]{1,0:T(8,128)S(1)} %get-tuple-element.84, f32[1024]{0:T(1024)S(1)} %bitcast.246, f32[1024]{0:T(1024)S(1)} %bitcast.212, ...), kind=kOutput, calls=%fused_computation.39 | convolution fusion | flops 4366794752 | bytes 23097344 | tf_op jit(solution)/shard_map/dot_general | solution.py:66
  442.7 8.8 fusion.140
  456.2 19.0 %convert_reduce_fusion = (f32[4096]{0:T(1024)}, bf16[512,4096]{1,0:T(8,128)(2,1)S(1)}) fusion(f32[512,4096]{1,0:T(8,128)} %get-tuple-element.86, f32[4096]{0:T(1024)S(1)} %bitcast.239, bf16[1024,12288]{1,0:T(8,128)(2,1)} %all-gather.6.cloned.1.call-done, f32[512,1024]{1,0:T(8,128)S(1)} %get-tuple-element.36), kind=kOutput, calls=%fused_computation.35 | convolution fusion | flops 4379373568 | bytes 23101440 | tf_op jit(solution)/shard_map/dot_general | solution.py:66
  475.2 9.7 multiply_reduce_fusion.2
  491.0 11.8 multiply_reduce_fusion.1
  502.8 12.6 multiply_convert_fusion.1
  537.5 19.3 %convert_reduce_fusion.1 = (f32[4096]{0:T(1024)}, bf16[512,4096]{1,0:T(8,128)(2,1)S(1)}) fusion(f32[512,4096]{1,0:T(8,128)} %get-tuple-element.78, f32[4096]{0:T(1024)S(1)} %bitcast.237, bf16[1024,12288]{1,0:T(8,128)(2,1)} %all-gather.4.cloned.1.call-done, f32[512,1024]{1,0:T(8,128)S(1)} %get-tuple-element.32), kind=kOutput, calls=%fused_computation.36 | convolution fusion | flops 4379373568 | bytes 23101440 | tf_op jit(solution)/shard_map/dot_general | solution.py:66
  556.8 9.1 multiply_reduce_fusion.4
  573.4 12.1 multiply_reduce_fusion
  585.5 12.6 multiply_convert_fusion
  627.6 9.4 convert_bitcast_fusion
  648.5 16.8 %pad_maximum_fusion = bf16[1024,12288]{1,0:T(8,128)(2,1)} fusion(bf16[1024,4096]{1,0:T(8,128)(2,1)} %convolution_convert_fusion.2, bf16[1024,4096]{1,0:T(8,128)(2,1)} %convolution_convert_fusion.3, bf16[1024,1024]{1,0:T(8,128)(2,1)S(1)} %copy.145, bf16[1024,3072]{1,0:T(8,128)(2,1)} %copy.144), kind=kLoop, calls=%fused_computation.2 | loop fusion | flops 100663296 | bytes 50331648 | tf_op jit(solution)/shard_map/concatenate | solution.py:239
  697.0 19.4 %pad_maximum_fusion.1 = bf16[1024,12288]{1,0:T(8,128)(2,1)} fusion(bf16[1024,4096]{1,0:T(8,128)(2,1)} %convolution_convert_fusion, bf16[1024,4096]{1,0:T(8,128)(2,1)} %convolution_convert_fusion.1, bf16[1024,1024]{1,0:T(8,128)(2,1)S(1)} %copy-done.19, bf16[1024,3072]{1,0:T(8,128)(2,1)} %convolution_convert_fusion.4), kind=kLoop, calls=%fused_computation.3 | loop fusion | flops 100663296 | bytes 50331648 | tf_op jit(solution)/shard_map/concatenate | solution.py:239
  717.9 193.0 %reduce-scatter.3.cloned.1.call-done = bf16[32,12288]{1,0:T(8,128)(2,1)} async-done(((bf16[1024,12288]{1,0:T(8,128)(2,1)}), bf16[32,12288]{1,0:T(8,128)(2,1)}) %reduce-scatter.3.cloned.1.call-update) | async-done | bytes 786448 | tf_op jit(solution)/shard_map/reduce_scatter | solution.py:240
  913.0 250.4 %reduce-scatter.5.cloned.1.call-done = bf16[32,12288]{1,0:T(8,128)(2,1)} async-done(((bf16[1024,12288]{1,0:T(8,128)(2,1)}), bf16[32,12288]{1,0:T(8,128)(2,1)}) %reduce-scatter.5.cloned.1.call-update) | async-done | bytes 786448 | tf_op jit(solution)/shard_map/reduce_scatter | solution.py:240
  1183.6 9.2 fusion.80
  1192.8 122.3 %all-reduce.2.cloned.1.call-done = f32[2,2,6,1024]{3,1,2,0:T(2,128)} async-done(((f32[2,2,6,1024]{3,1,2,0:T(2,128)}), f32[2,2,6,1024]{3,1,2,0:T(2,128)}) %all-reduce.2.cloned.1.call-update) | async-done | bytes 98320 | tf_op jit(solution)/shard_map/psum | solution.py:254
  (334 shorter events, 237.0 us)
Async XLA Ops:
  7.2 74.2 %copy-start = (s32[4,512]{1,0:T(4,128)S(1)}, s32[4,512]{1,0:T(4,128)}, u32[]{:S(2)}) copy-start(s32[4,512]{1,0:T(4,128)} %param.10) | copy-start | bytes 24580
  11.2 52.7 %all-to-all-start = ((bf16[32,4,32,256]{3,2,1,0:T(8,128)(2,1)}), bf16[32,4,32,256]{3,2,1,0:T(8,128)(2,1)S(1)}, u32[]{:S(2)}, u32[]{:S(2)}) async-start(bf16[32,4,32,256]{3,2,1,0:T(8,128)(2,1)} %copy.127), calls=%async_computation | async-start | bytes 4194304 | tf_op jit(solution)/shard_map/all_to_all | solution.py:97
  17.2 211.9 %all-gather.4.cloned.1.call-start = ((), (), s32[]{:S(2)}) async-start(), calls=%async_computation.4 | async-start | bytes 25952256 | tf_op jit(solution)/shard_map/all_gather | solution.py:104
  72.2 156.9 %copy-start.86 = (bf16[512,1024]{1,0:T(8,128)(2,1)S(1)}, bf16[512,1024]{1,0:T(8,128)(2,1)}, u32[]{:S(2)}) copy-start(bf16[512,1024]{1,0:T(8,128)(2,1)} %param.9) | copy-start | bytes 3145732
  74.8 310.6 %all-gather.6.cloned.1.call-start = ((), (), s32[]{:S(2)}) async-start(), calls=%async_computation.5 | async-start | bytes 25952256 | tf_op jit(solution)/shard_map/all_gather | solution.py:104
  75.8 835.1 %reduce-scatter.3.cloned.1.call-start = ((), (), s32[]{:S(2)}) async-start(), calls=%async_computation.6 | async-start | bytes 25952256 | tf_op jit(solution)/shard_map/reduce_scatter | solution.py:240
  82.9 200.0 %copy-start.62 = (f32[1,1,1,1024]{3,1,2,0:T(1,128)}, f32[1,1,1,1024]{3,1,2,0:T(1,128)S(1)}, u32[]{:S(2)}) copy-start(f32[1,1,1,1024]{3,1,2,0:T(1,128)S(1)} %get-tuple-element.58) | copy-start | bytes 12292
  82.9 200.0 %copy-start.84 = (f32[1,1,1,1024]{3,1,2,0:T(1,128)}, f32[1,1,1,1024]{3,1,2,0:T(1,128)S(1)}, u32[]{:S(2)}) copy-start(f32[1,1,1,1024]{3,1,2,0:T(1,128)S(1)} %get-tuple-element.57) | copy-start | bytes 12292
  82.9 337.2 %copy-start.59 = (f32[1,1,1,1024]{3,1,2,0:T(1,128)}, f32[1,1,1,1024]{3,1,2,0:T(1,128)S(1)}, u32[]{:S(2)}) copy-start(f32[1,1,1,1024]{3,1,2,0:T(1,128)S(1)} %get-tuple-element.55) | copy-start | bytes 12292
  82.9 337.2 %copy-start.82 = (f32[1,1,1,1024]{3,1,2,0:T(1,128)}, f32[1,1,1,1024]{3,1,2,0:T(1,128)S(1)}, u32[]{:S(2)}) copy-start(f32[1,1,1,1024]{3,1,2,0:T(1,128)S(1)} %get-tuple-element.54) | copy-start | bytes 12292
  82.9 359.8 %copy-start.80 = (f32[1,1,1,1024]{3,1,2,0:T(1,128)}, f32[1,1,1,1024]{3,1,2,0:T(1,128)S(1)}, u32[]{:S(2)}) copy-start(f32[1,1,1,1024]{3,1,2,0:T(1,128)S(1)} %get-tuple-element.51) | copy-start | bytes 12292
  83.0 402.0 %copy-start.57 = (f32[1,1,1,1024]{3,1,2,0:T(1,128)}, f32[1,1,1,1024]{3,1,2,0:T(1,128)S(1)}, u32[]{:S(2)}) copy-start(f32[1,1,1,1024]{3,1,2,0:T(1,128)S(1)} %get-tuple-element.52) | copy-start | bytes 12292
  83.0 181.6 %copy-start.67 = (f32[1,4,1024]{2,0,1:T(1,128)}, f32[1,4,1024]{2,0,1:T(1,128)S(1)}, u32[]{:S(2)}) copy-start(f32[1,4,1024]{2,0,1:T(1,128)S(1)} %get-tuple-element.64) | copy-start | bytes 49156
  291.7 99.5 %copy-start.11 = (f32[512,1024]{1,0:T(8,128)}, f32[512,1024]{1,0:T(8,128)S(1)}, u32[]{:S(2)}) copy-start(f32[512,1024]{1,0:T(8,128)S(1)} %get-tuple-element.80) | copy-start | bytes 6291460
  291.7 128.4 %copy-start.45 = (f32[512]{0:T(512)}, f32[512]{0:T(512)S(1)}, u32[]{:S(2)}) copy-start(f32[512]{0:T(512)S(1)} %broadcast_multiply_fusion.10) | copy-start | bytes 6148
  292.1 128.1 %copy-start.69 = (f32[512]{0:T(512)}, f32[512]{0:T(512)S(1)}, u32[]{:S(2)}) copy-start(f32[512]{0:T(512)S(1)} %add_rsqrt_fusion.2) | copy-start | bytes 6148
  424.0 60.9 %copy-start.17 = (f32[512,1024]{1,0:T(8,128)}, f32[512,1024]{1,0:T(8,128)S(1)}, u32[]{:S(2)}) copy-start(f32[512,1024]{1,0:T(8,128)S(1)} %get-tuple-element.84) | copy-start | bytes 6291460
  424.0 60.9 %copy-start.50 = (f32[512]{0:T(512)}, f32[512]{0:T(512)S(1)}, u32[]{:S(2)}) copy-start(f32[512]{0:T(512)S(1)} %broadcast_multiply_fusion.9) | copy-start | bytes 6148
  424.4 60.6 %copy-start.74 = (f32[512]{0:T(512)}, f32[512]{0:T(512)S(1)}, u32[]{:S(2)}) copy-start(f32[512]{0:T(512)S(1)} %add_rsqrt_fusion.1) | copy-start | bytes 6148
  665.4 498.1 %reduce-scatter.5.cloned.1.call-start = ((), (), s32[]{:S(2)}) async-start(), calls=%async_computation.7 | async-start | bytes 25952256 | tf_op jit(solution)/shard_map/reduce_scatter | solution.py:240
  1172.9 144.7 %all-to-all-start.1 = ((bf16[32,4,32,256]{3,2,1,0:T(8,128)(2,1)}), bf16[32,4,32,256]{3,2,1,0:T(8,128)(2,1)S(1)}, u32[]{:S(2)}, u32[]{:S(2)}) async-start(bf16[32,4,32,256]{3,2,1,0:T(8,128)(2,1)} %bitcast.167), calls=%async_computation.3 | async-start | bytes 4194304 | tf_op jit(solution)/shard_map/all_to_all | solution.py:267
  1177.4 137.7 %all-reduce.2.cloned.1.call-start = ((), (), s32[]{:S(2)}) async-start(), calls=%async_computation.8 | async-start | bytes 196608 | tf_op jit(solution)/shard_map/psum | solution.py:254
  1183.6 131.6 %copy-start.42 = (f32[3,2,6,1024]{3,1,2,0:T(2,128)S(1)}, f32[3,2,6,1024]{3,1,2,0:T(2,128)}, u32[]{:S(2)}) copy-start(f32[3,2,6,1024]{3,1,2,0:T(2,128)} %param.16) | copy-start | bytes 442372
  1183.6 132.5 %copy-start.43 = (f32[3,2,6,256]{3,1,2,0:T(2,128)S(1)}, f32[3,2,6,256]{3,1,2,0:T(2,128)}, u32[]{:S(2)}) copy-start(f32[3,2,6,256]{3,1,2,0:T(2,128)} %param.15) | copy-start | bytes 110596
  (86 other events, 808.8 us)
Sparse Core Ops, SparseCore 0:
  74.9 154.1 all-gather.3
  232.6 152.7 all-gather.5
  665.4 245.4 reduce-scatter.2
  918.4 245.0 reduce-scatter.4
  1184.1 130.9 all-reduce.1
where the time goes:
time: 1340 us
  waiting for transfers between devices  852 us (64%)
  matrix products  289 us (22%)
  other arithmetic  115 us (9%)
  local copies, waits for them, and re-layouts  51.2 us (4%)
  between operations  15.6 us (1%)
    reduce_scatter x2, waiting for transfers between devices, local(): lax.psum_scatter(whole.astype(jnp.bfloat16), BOTH, scatter_dimension=0, t...  443 us
    all_gather x2, waiting for transfers between devices, local(): lax.all_gather(own.reshape(piece, per_layer * width), BOTH, axis=0, tiled...  239 us
    dot_general x24, matrix products, dot(): lax.dot_general(left, right, (dims, ((), ())), preferred_element_type=jnp...  208 us
    psum x1, waiting for transfers between devices, local(): lax.psum(jnp.stack([jnp.stack(col_parts), jnp.stack(row_parts)]), BOTH)  122 us
    all_to_all x1, waiting for transfers between devices, local(): spread = lax.all_to_all(sent.transpose(1, 0, 2, 3), BOTH, 0, 0)  46.5 us
    concatenate x2, other arithmetic, local(): jnp.concatenate([grad_w_qkv, grad_w_proj, grad_w_in, grad_w_out], axis=1)  36.2 us
  transfers between devices with their start and end apart: 7, of which 6 were waited for; matrix products, arithmetic and copies ran while one was open for 10% of the time, Pallas kernels for 0%

commit v1 on v0

--- a/solution.py
+++ b/solution.py
@@ -3,6 +3,7 @@
 import jax.numpy as jnp
 from jax import lax
 from jax.sharding import PartitionSpec as P
+from jax.lax import all_gather
 
 HEAD_DIM = 64
 LAYERS = 2
@@ -14,6 +15,11 @@
 ADAM_EPS = 1e-08
 BETA_MOMENT = 0.5
 BOTH = ("dp", "tensor")
+
+
+def proceed_local_data(q_in, comm_axis):
+    o_now = jnp.sum(all_gather(q_in, axis_name=comm_axis), axis=0)
+    return o_now
 
 
 def norm_forward(summed, gain, shift):
@@ -251,7 +257,9 @@
         row_parts[layer] = jnp.stack(
             [grad_bias_proj, grad_bias_two, gain_one, shift_one, gain_two, shift_two]
         )
-    small = lax.psum(jnp.stack([jnp.stack(col_parts), jnp.stack(row_parts)]), BOTH)
+    small = proceed_local_data(
+        jnp.stack([jnp.stack(col_parts), jnp.stack(row_parts)]), comm_axis=BOTH
+    )
     row_total = small[1]
     col_total = lax.dynamic_slice_in_dim(small[0], tensor_index * col_width, col_width, axis=2)
     summed = jnp.concatenate(

time: 1340 us -> 1270 us (0.948)
  waiting for transfers between devices: 852 us -> 772 us
    psum x1 -> x0, waiting for transfers between devices: 122 us -> none  [local(): lax.psum(jnp.stack([jnp.stack(col_parts), jnp.stack(row_parts)]), BOTH)]
    all_gather x0 -> x1, waiting for transfers between devices: none -> 48.7 us  [proceed_local_data(): o_now = jnp.sum(all_gather(q_in, axis_name=comm_axis), axis=0)]
  transfers between devices with their start and end apart: 7 -> 7, of which waited for: 6 -> 6; matrix products, arithmetic and copies ran while one was open for 10% -> 12% of each run, Pallas kernels for 0% -> 0%
where the time goes in v1:
time: 1270 us; the launch traced here: 1260 us
  waiting for transfers between devices  772 us (61%)
  matrix products  288 us (23%)
  other arithmetic  116 us (9%)
  local copies, waits for them, and re-layouts  50.8 us (4%)
  between operations  15.7 us (1%)
    reduce_scatter x2, waiting for transfers between devices, local(): lax.psum_scatter(whole.astype(jnp.bfloat16), BOTH, scatter_dimension=0, t...  438 us
    all_gather x2, waiting for transfers between devices, local(): lax.all_gather(own.reshape(piece, per_layer * width), BOTH, axis=0, tiled...  239 us
    dot_general x24, matrix products, dot(): lax.dot_general(left, right, (dims, ((), ())), preferred_element_type=jnp...  207 us
    all_gather x1, waiting for transfers between devices, proceed_local_data(): o_now = jnp.sum(all_gather(q_in, axis_name=comm_axis), axis=0)  48.7 us
    all_to_all x1, waiting for transfers between devices, local(): spread = lax.all_to_all(sent.transpose(1, 0, 2, 3), BOTH, 0, 0)  46.5 us
    concatenate x2, other arithmetic, local(): jnp.concatenate([grad_w_qkv, grad_w_proj, grad_w_in, grad_w_out], axis=1)  36.1 us
  transfers between devices with their start and end apart: 7, of which 6 were waited for; matrix products, arithmetic and copies ran while one was open for 12% of the time, Pallas kernels for 0%

profile of v1, /device:TPU:8, one launch (start us, length us, event | category | flops | bytes accessed | tf_op | source)
XLA Modules:
  0.0 1258.8 jit_solution(1376501526680302810)
XLA Ops:
  17.3 46.5 %all-to-all-done = bf16[32,4,32,256]{3,2,1,0:T(8,128)(2,1)S(1)} async-done(((bf16[32,4,32,256]{3,2,1,0:T(8,128)(2,1)}), bf16[32,4,32,256]{3,2,1,0:T(8,128)(2,1)S(1)}, u32[]{:S(2)}, u32[]{:S(2)}) %all-to-all-start) | async-done | bytes 2097184 | tf_op jit(solution)/shard_map/all_to_all | solution.py:103
  83.2 145.9 %all-gather.6.cloned.1.call-done = bf16[1024,12288]{1,0:T(8,128)(2,1)} async-done(((bf16[32,12288]{1,0:T(8,128)(2,1)}), bf16[1024,12288]{1,0:T(8,128)(2,1)}) %all-gather.6.cloned.1.call-update) | async-done | bytes 25165840 | tf_op jit(solution)/shard_map/all_gather | solution.py:110
  242.9 9.4 exponential_reduce_fusion.1
  264.6 18.3 %multiply_convert_fusion.5 = (bf16[512,4096]{1,0:T(8,128)(2,1)S(1)}, f32[512,4096]{1,0:T(8,128)}) fusion(f32[4096]{0:T(1024)S(1)} %bitcast.238, bf16[1024,12288]{1,0:T(8,128)(2,1)} %all-gather.6.cloned.1.call-done, f32[512,1024]{1,0:T(8,128)S(1)} %get-tuple-element.76, f32[1024]{0:T(1024)S(1)} %bitcast.254, f32[1024]{0:T(1024)S(1)} %bitcast.224, ...), kind=kOutput, calls=%fused_computation.40 | convolution fusion | flops 4366794752 | bytes 23097344 | tf_op jit(solution)/shard_map/dot_general | solution.py:72
  292.1 93.3 %all-gather.8.cloned.1.call-done = bf16[1024,12288]{1,0:T(8,128)(2,1)} async-done(((bf16[32,12288]{1,0:T(8,128)(2,1)}), bf16[1024,12288]{1,0:T(8,128)(2,1)}) %all-gather.8.cloned.1.call-update) | async-done | bytes 25165840 | tf_op jit(solution)/shard_map/all_gather | solution.py:110
  401.8 9.5 exponential_reduce_fusion
  424.4 18.3 %multiply_convert_fusion.4 = (bf16[512,4096]{1,0:T(8,128)(2,1)S(1)}, f32[512,4096]{1,0:T(8,128)}) fusion(f32[4096]{0:T(1024)S(1)} %bitcast.240, bf16[1024,12288]{1,0:T(8,128)(2,1)} %all-gather.8.cloned.1.call-done, f32[512,1024]{1,0:T(8,128)S(1)} %get-tuple-element.84, f32[1024]{0:T(1024)S(1)} %bitcast.248, f32[1024]{0:T(1024)S(1)} %bitcast.214, ...), kind=kOutput, calls=%fused_computation.39 | convolution fusion | flops 4366794752 | bytes 23097344 | tf_op jit(solution)/shard_map/dot_general | solution.py:72
  442.8 8.8 fusion.140
  456.2 19.0 %convert_reduce_fusion = (f32[4096]{0:T(1024)}, bf16[512,4096]{1,0:T(8,128)(2,1)S(1)}) fusion(f32[512,4096]{1,0:T(8,128)} %get-tuple-element.86, f32[4096]{0:T(1024)S(1)} %bitcast.241, bf16[1024,12288]{1,0:T(8,128)(2,1)} %all-gather.8.cloned.1.call-done, f32[512,1024]{1,0:T(8,128)S(1)} %get-tuple-element.36), kind=kOutput, calls=%fused_computation.35 | convolution fusion | flops 4379373568 | bytes 23101440 | tf_op jit(solution)/shard_map/dot_general | solution.py:72
  475.2 9.7 multiply_reduce_fusion.2
  491.0 11.8 multiply_reduce_fusion.1
  502.8 12.6 multiply_convert_fusion.1
  537.4 18.7 %convert_reduce_fusion.1 = (f32[4096]{0:T(1024)S(1)}, bf16[512,4096]{1,0:T(8,128)(2,1)S(1)}) fusion(f32[512,4096]{1,0:T(8,128)} %get-tuple-element.78, f32[4096]{0:T(1024)S(1)} %bitcast.239, bf16[1024,12288]{1,0:T(8,128)(2,1)} %all-gather.6.cloned.1.call-done, f32[512,1024]{1,0:T(8,128)S(1)} %get-tuple-element.32), kind=kOutput, calls=%fused_computation.36 | convolution fusion | flops 4379373568 | bytes 23101440 | tf_op jit(solution)/shard_map/dot_general | solution.py:72
  556.3 9.1 multiply_reduce_fusion.4
  572.8 12.4 multiply_reduce_fusion
  585.1 12.6 %multiply_convert_fusion = bf16[16,512,512]{1,2,0:T(8,128)(2,1)S(1)} fusion(f32[16,512,512]{1,2,0:T(8,128)} %get-tuple-element.95, f32[16,512,512]{1,2,0:T(8,128)} %get-tuple-element.74, f32[16,512]{1,0:T(8,128)S(1)} %get-tuple-element.94, f32[16,512]{1,0:T(8,128)S(1)} %copy-done.43, pred[512,512]{0,1:T(8,128)(4,1)S(1)} %broadcast_compare_fusion), kind=kLoop, calls=%fused_computation.4 | loop fusion | flops 25165824 | bytes 42270720 | tf_op jit(solution)/shard_map/convert_element_type | solution.py:223
  627.1 9.4 convert_bitcast_fusion
  648.0 16.8 %pad_maximum_fusion = bf16[1024,12288]{1,0:T(8,128)(2,1)} fusion(bf16[1024,4096]{1,0:T(8,128)(2,1)} %convolution_convert_fusion.2, bf16[1024,4096]{1,0:T(8,128)(2,1)} %convolution_convert_fusion.3, bf16[1024,1024]{1,0:T(8,128)(2,1)S(1)} %copy.145, bf16[1024,3072]{1,0:T(8,128)(2,1)} %copy.144), kind=kLoop, calls=%fused_computation.2 | loop fusion | flops 100663296 | bytes 50331648 | tf_op jit(solution)/shard_map/concatenate | solution.py:245
  673.5 9.1 convolution_convert_fusion.4
  696.9 19.3 %pad_maximum_fusion.1 = bf16[1024,12288]{1,0:T(8,128)(2,1)} fusion(bf16[1024,4096]{1,0:T(8,128)(2,1)} %convolution_convert_fusion, bf16[1024,4096]{1,0:T(8,128)(2,1)} %convolution_convert_fusion.1, bf16[1024,1024]{1,0:T(8,128)(2,1)S(1)} %copy-done.19, bf16[1024,3072]{1,0:T(8,128)(2,1)} %convolution_convert_fusion.4), kind=kLoop, calls=%fused_computation.3 | loop fusion | flops 100663296 | bytes 50331648 | tf_op jit(solution)/shard_map/concatenate | solution.py:245
  724.0 186.4 %reduce-scatter.3.cloned.1.call-done = bf16[32,12288]{1,0:T(8,128)(2,1)} async-done(((bf16[1024,12288]{1,0:T(8,128)(2,1)}), bf16[32,12288]{1,0:T(8,128)(2,1)}) %reduce-scatter.3.cloned.1.call-update) | async-done | bytes 786448 | tf_op jit(solution)/shard_map/reduce_scatter | solution.py:246
  911.6 251.3 %reduce-scatter.5.cloned.1.call-done = bf16[32,12288]{1,0:T(8,128)(2,1)} async-done(((bf16[1024,12288]{1,0:T(8,128)(2,1)}), bf16[32,12288]{1,0:T(8,128)(2,1)}) %reduce-scatter.5.cloned.1.call-update) | async-done | bytes 786448 | tf_op jit(solution)/shard_map/reduce_scatter | solution.py:246
  1175.7 8.8 fusion.80
  1184.6 48.7 %all-gather.10.cloned.1.call-done = f32[64,2,6,1024]{3,1,2,0:T(2,128)} async-done(((f32[2,2,6,1024]{3,1,2,0:T(2,128)}), f32[64,2,6,1024]{3,1,2,0:T(2,128)}) %all-gather.10.cloned.1.call-update) | async-done | bytes 3145744 | tf_op jit(solution)/shard_map/all_gather | solution.py:21
  (337 shorter events, 237.2 us)
Async XLA Ops:
  7.2 74.2 %copy-start = (s32[4,512]{1,0:T(4,128)S(1)}, s32[4,512]{1,0:T(4,128)}, u32[]{:S(2)}) copy-start(s32[4,512]{1,0:T(4,128)} %param.10) | copy-start | bytes 24580
  11.2 52.7 %all-to-all-start = ((bf16[32,4,32,256]{3,2,1,0:T(8,128)(2,1)}), bf16[32,4,32,256]{3,2,1,0:T(8,128)(2,1)S(1)}, u32[]{:S(2)}, u32[]{:S(2)}) async-start(bf16[32,4,32,256]{3,2,1,0:T(8,128)(2,1)} %copy.127), calls=%async_computation | async-start | bytes 4194304 | tf_op jit(solution)/shard_map/all_to_all | solution.py:103
  17.2 211.9 %all-gather.6.cloned.1.call-start = ((), (), s32[]{:S(2)}) async-start(), calls=%async_computation.4 | async-start | bytes 25952256 | tf_op jit(solution)/shard_map/all_gather | solution.py:110
  72.2 156.9 %copy-start.87 = (bf16[512,1024]{1,0:T(8,128)(2,1)S(1)}, bf16[512,1024]{1,0:T(8,128)(2,1)}, u32[]{:S(2)}) copy-start(bf16[512,1024]{1,0:T(8,128)(2,1)} %param.9) | copy-start | bytes 3145732
  74.8 310.6 %all-gather.8.cloned.1.call-start = ((), (), s32[]{:S(2)}) async-start(), calls=%async_computation.5 | async-start | bytes 25952256 | tf_op jit(solution)/shard_map/all_gather | solution.py:110
  75.8 834.6 %reduce-scatter.3.cloned.1.call-start = ((), (), s32[]{:S(2)}) async-start(), calls=%async_computation.6 | async-start | bytes 25952256 | tf_op jit(solution)/shard_map/reduce_scatter | solution.py:246
  82.9 200.0 %copy-start.64 = (f32[1,1,1,1024]{3,1,2,0:T(1,128)}, f32[1,1,1,1024]{3,1,2,0:T(1,128)S(1)}, u32[]{:S(2)}) copy-start(f32[1,1,1,1024]{3,1,2,0:T(1,128)S(1)} %get-tuple-element.58) | copy-start | bytes 12292
  82.9 200.0 %copy-start.85 = (f32[1,1,1,1024]{3,1,2,0:T(1,128)}, f32[1,1,1,1024]{3,1,2,0:T(1,128)S(1)}, u32[]{:S(2)}) copy-start(f32[1,1,1,1024]{3,1,2,0:T(1,128)S(1)} %get-tuple-element.57) | copy-start | bytes 12292
  82.9 337.2 %copy-start.61 = (f32[1,1,1,1024]{3,1,2,0:T(1,128)}, f32[1,1,1,1024]{3,1,2,0:T(1,128)S(1)}, u32[]{:S(2)}) copy-start(f32[1,1,1,1024]{3,1,2,0:T(1,128)S(1)} %get-tuple-element.55) | copy-start | bytes 12292
  82.9 337.2 %copy-start.83 = (f32[1,1,1,1024]{3,1,2,0:T(1,128)}, f32[1,1,1,1024]{3,1,2,0:T(1,128)S(1)}, u32[]{:S(2)}) copy-start(f32[1,1,1,1024]{3,1,2,0:T(1,128)S(1)} %get-tuple-element.54) | copy-start | bytes 12292
  82.9 359.8 %copy-start.81 = (f32[1,1,1,1024]{3,1,2,0:T(1,128)}, f32[1,1,1,1024]{3,1,2,0:T(1,128)S(1)}, u32[]{:S(2)}) copy-start(f32[1,1,1,1024]{3,1,2,0:T(1,128)S(1)} %get-tuple-element.51) | copy-start | bytes 12292
  83.0 402.0 %copy-start.59 = (f32[1,1,1,1024]{3,1,2,0:T(1,128)}, f32[1,1,1,1024]{3,1,2,0:T(1,128)S(1)}, u32[]{:S(2)}) copy-start(f32[1,1,1,1024]{3,1,2,0:T(1,128)S(1)} %get-tuple-element.52) | copy-start | bytes 12292
  83.0 181.6 %copy-start.68 = (f32[1,4,1024]{2,0,1:T(1,128)}, f32[1,4,1024]{2,0,1:T(1,128)S(1)}, u32[]{:S(2)}) copy-start(f32[1,4,1024]{2,0,1:T(1,128)S(1)} %get-tuple-element.64) | copy-start | bytes 49156
  291.7 99.5 %copy-start.11 = (f32[512,1024]{1,0:T(8,128)}, f32[512,1024]{1,0:T(8,128)S(1)}, u32[]{:S(2)}) copy-start(f32[512,1024]{1,0:T(8,128)S(1)} %get-tuple-element.80) | copy-start | bytes 6291460
  291.7 128.4 %copy-start.47 = (f32[512]{0:T(512)}, f32[512]{0:T(512)S(1)}, u32[]{:S(2)}) copy-start(f32[512]{0:T(512)S(1)} %broadcast_multiply_fusion.10) | copy-start | bytes 6148
  292.1 128.1 %copy-start.70 = (f32[512]{0:T(512)}, f32[512]{0:T(512)S(1)}, u32[]{:S(2)}) copy-start(f32[512]{0:T(512)S(1)} %add_rsqrt_fusion.2) | copy-start | bytes 6148
  424.0 60.9 %copy-start.17 = (f32[512,1024]{1,0:T(8,128)}, f32[512,1024]{1,0:T(8,128)S(1)}, u32[]{:S(2)}) copy-start(f32[512,1024]{1,0:T(8,128)S(1)} %get-tuple-element.84) | copy-start | bytes 6291460
  424.0 60.9 %copy-start.52 = (f32[512]{0:T(512)}, f32[512]{0:T(512)S(1)}, u32[]{:S(2)}) copy-start(f32[512]{0:T(512)S(1)} %broadcast_multiply_fusion.9) | copy-start | bytes 6148
  424.4 60.6 %copy-start.75 = (f32[512]{0:T(512)}, f32[512]{0:T(512)S(1)}, u32[]{:S(2)}) copy-start(f32[512]{0:T(512)S(1)} %add_rsqrt_fusion.1) | copy-start | bytes 6148
  664.9 498.0 %reduce-scatter.5.cloned.1.call-start = ((), (), s32[]{:S(2)}) async-start(), calls=%async_computation.7 | async-start | bytes 25952256 | tf_op jit(solution)/shard_map/reduce_scatter | solution.py:246
  716.4 516.9 %all-gather.10.cloned.1.call-start = ((), (), s32[]{:S(2)}) async-start(), calls=%async_computation.8 | async-start | bytes 3244032 | tf_op jit(solution)/shard_map/all_gather | solution.py:21
  1171.2 66.9 %all-to-all-start.1 = ((bf16[32,4,32,256]{3,2,1,0:T(8,128)(2,1)}), bf16[32,4,32,256]{3,2,1,0:T(8,128)(2,1)S(1)}, u32[]{:S(2)}, u32[]{:S(2)}) async-start(bf16[32,4,32,256]{3,2,1,0:T(8,128)(2,1)} %bitcast.168), calls=%async_computation.3 | async-start | bytes 4194304 | tf_op jit(solution)/shard_map/all_to_all | solution.py:275
  1175.7 60.7 %copy-start.44 = (f32[3,2,6,1024]{3,1,2,0:T(2,128)S(1)}, f32[3,2,6,1024]{3,1,2,0:T(2,128)}, u32[]{:S(2)}) copy-start(f32[3,2,6,1024]{3,1,2,0:T(2,128)} %param.16) | copy-start | bytes 442372
  1175.7 60.9 %copy-start.45 = (f32[3,2,6,256]{3,1,2,0:T(2,128)S(1)}, f32[3,2,6,256]{3,1,2,0:T(2,128)}, u32[]{:S(2)}) copy-start(f32[3,2,6,256]{3,1,2,0:T(2,128)} %param.15) | copy-start | bytes 110596
  (87 other events, 746.8 us)
Sparse Core Ops, SparseCore 0:
  74.9 154.1 all-gather.5
  232.6 152.7 all-gather.7
  664.9 245.4 reduce-scatter.2
  917.8 244.9 reduce-scatter.4
  1166.2 67.1 all-gather.9
